TPU v7x, 32 devices: a whole 2x2x4 slice. The times are simulated.
32 devices in a mesh: ch: 16 (over z, x, core), rep: 2 (over y).
Axes of the slice: x: 2, y: 2, z: 4, core: 2. Of those that a mesh axis runs over, the one named last changes fastest.
Arguments:
- fields_a: bfloat16 [32, 128, 4096], P('rep', 'ch'), parts along dimension 0, may hold values from -6 to 6
- latent_b: bfloat16 [32, 2048, 512], P('rep', 'ch'), parts along dimension 0, may hold values from -6 to 6
- regrid_w: bfloat16 [32, 1, 128, 64], replicated, may hold values from -0.5 to 0.5
- cell_tiles: int32 [32, 1], replicated, may hold values from 0 to 31, as said below
- norm_a: float32 [128], replicated, may hold values from 0.5 to 1.5
- enc_in: bfloat16 [128, 512], replicated, may hold values from -0.5 to 0.5
- enc_mid: bfloat16 [512, 512], replicated, may hold values from -0.25 to 0.25
- enc_out: bfloat16 [512, 512], replicated, may hold values from -0.25 to 0.25
- norm_b: float32 [512], replicated, may hold values from 0.5 to 1.5
- dec_mid: bfloat16 [512, 512], replicated, may hold values from -0.25 to 0.25
- dec_out: bfloat16 [512, 128], replicated, may hold values from -0.25 to 0.25
Outputs:
- latent_a: bfloat16 [32, 2048, 512], P('rep', 'ch'), parts along dimension 0
- cells_b: bfloat16 [32, 128, 4096], P('rep', 'ch'), parts along dimension 0
There are 2 independent parts, one for each index of `rep`. A program takes and returns all parts, laid end to end along the dimension named above; an argument that names none is the same for every part. Nothing has to cross between parts.
Inputs may be any that keep to these rules, and one draw needn't show every extreme that they name: The one column of cell_tiles names every one of the 32 cell blocks exactly once.
All inputs are finite; a program needn't handle non-finite values.
Results may differ from a plain program's by a relative error of at most 0.0066.
Values may be sent and summed in bfloat16 or wider, within the bound.
A program may use at most 64 MiB of HBM per device.

v0:
```python
import jax
import jax.numpy as jnp
from jax import lax
from jax.sharding import PartitionSpec as P

BN = 64
BC = 128
K = 1
EPSILON = 1e-05


def normalize(values, gain_vec, along):
    average = jnp.mean(values, axis=along, keepdims=True)
    centred = values - average
    spread = jnp.mean(centred * centred, axis=along, keepdims=True)
    return centred * lax.rsqrt(spread + EPSILON) * gain_vec


def shards(
    fields_a,
    latent_b,
    regrid_w,
    cell_tiles,
    norm_a,
    enc_in,
    enc_mid,
    enc_out,
    norm_b,
    dec_mid,
    dec_out,
):
    groups = lax.axis_size("ch")
    samples = fields_a.shape[0]
    own_channels = fields_a.shape[1]
    blocks_all = cell_tiles.shape[0]
    node_rows = latent_b.shape[1]
    hidden = latent_b.shape[2]
    channels = own_channels * groups
    blocks = fields_a.reshape(samples, own_channels, blocks_all, BC)
    chosen = jnp.take(blocks, cell_tiles, axis=2).reshape(samples, own_channels, blocks_all, K * BC)
    weights = regrid_w.reshape(blocks_all, K * BC, BN)
    grid_vals = jnp.einsum("ecnj,njm->ecnm", chosen, weights, preferred_element_type=jnp.float32)
    grid_sent = grid_vals.astype(jnp.bfloat16).reshape(samples, own_channels, groups, node_rows)
    received_a = lax.all_to_all(grid_sent, "ch", split_axis=2, concat_axis=1, tiled=True)
    normed = normalize(latent_b.astype(jnp.float32), norm_b, 2).astype(jnp.bfloat16)
    middle = jax.nn.silu(
        jnp.einsum("enh,hg->eng", normed, dec_mid, preferred_element_type=jnp.float32)
    ).astype(jnp.bfloat16)
    out_split = dec_out.reshape(hidden, groups, own_channels)
    decoded_sent = jnp.einsum(
        "enh,hjc->ecjn", middle, out_split, preferred_element_type=jnp.float32
    ).astype(jnp.bfloat16)
    values = received_a.reshape(samples, channels, node_rows).astype(jnp.float32)
    normed = normalize(values, norm_a[:, None], 1).astype(jnp.bfloat16)
    base = jnp.einsum("ecn,ch->enh", normed, enc_in, preferred_element_type=jnp.float32).astype(
        jnp.bfloat16
    )
    middle = jax.nn.silu(
        jnp.einsum("enh,hg->eng", base, enc_mid, preferred_element_type=jnp.float32)
    ).astype(jnp.bfloat16)
    result = base.astype(jnp.float32) + jnp.einsum(
        "enh,hg->eng", middle, enc_out, preferred_element_type=jnp.float32
    )
    latent_a = result.astype(jnp.bfloat16)
    received_b = lax.all_to_all(decoded_sent, "ch", split_axis=2, concat_axis=1, tiled=True)
    arranged = received_b.reshape(samples, groups, own_channels, node_rows)
    node_blocks = jnp.moveaxis(arranged, 1, 2).reshape(samples, own_channels, blocks_all, BN)
    inverse = jnp.argsort(cell_tiles, axis=0).T
    picked = jnp.take(node_blocks, inverse, axis=2)
    weight_sel = regrid_w[inverse, jnp.arange(K)[:, None]]
    total = jnp.einsum("ecknm,knbm->ecnb", picked, weight_sel, preferred_element_type=jnp.float32)
    cells_b = total.astype(jnp.bfloat16).reshape(samples, own_channels, blocks_all * BC)
    return (latent_a, cells_b)


def solution(mesh):
    placed = (
        P("rep", "ch", None),
        P("rep", "ch", None),
        P(),
        P(),
        P(),
        P(),
        P(),
        P(),
        P(),
        P(),
        P(),
    )
    return jax.shard_map(
        shards,
        mesh=mesh,
        in_specs=placed,
        out_specs=(P("rep", "ch", None), P("rep", "ch", None)),
        check_vma=False,
    )
```

profile of v0, /device:TPU:0, one launch (start us, length us, event | category | flops | bytes accessed | tf_op | source)
XLA Modules:
  0.0 64.0 jit_solution(9747075597492145657)
XLA Ops:
  0.6 0.0 copy-start
  0.6 0.0 copy-start.2
  0.7 0.8 %fusion.60 = s32[32]{0:T(128)S(1)} fusion(s32[32,1]{0,1:T(1,128)} %param.14), kind=kLoop, calls=%fused_computation.72 | loop fusion | flops 96 | bytes 256 | tf_op jit(solution)/shard_map/jit(_take)/broadcast_in_dim | solution.py:40
  1.4 0.7 %and_bitcast_fusion = pred[32]{0:T(512)(128)(4,1)S(1)} fusion(s32[32,1]{0,1:T(1,128)} %param.14), kind=kLoop, calls=%fused_computation.66 | loop fusion | flops 192 | bytes 160 | tf_op jit(solution)/shard_map/jit(_take)/reduce_and | solution.py:40
  2.1 0.0 copy-done
  2.1 0.9 %gather_fusion = bf16[32,16,8,128]{3,2,1,0:T(8,128)(2,1)S(1)} fusion(bf16[16,8,32,128]{3,1,2,0:T(8,128)(2,1)S(1)} %bitcast.101, s32[1024]{0:T(1024)S(1)} %pad_clamp_fusion.1), kind=kCustom, calls=%fused_computation | custom fusion | bytes 2097280 | tf_op jit(solution)/shard_map/jit(_take)/gather | solution.py:40
  3.1 0.0 copy-done.2
  3.1 0.5 fusion.14
  3.6 1.6 %copy.42 = bf16[16,8,32,64]{3,2,1,0:T(8,128)(2,1)} copy(bf16[16,8,32,64]{3,1,0,2:T(8,128)(2,1)S(1)} %fusion.14) | data formatting | bytes 1048576 | tf_op jit(solution)/shard_map/convert_element_type | solution.py:43
  5.2 0.0 copy-start.1
  5.2 2.6 %reshape.150 = bf16[16,8,16,128]{3,2,1,0:T(8,128)(2,1)} reshape(bf16[16,8,32,64]{3,2,1,0:T(8,128)(2,1)} %copy.42) | data formatting | bytes 1048576 | tf_op jit(solution)/shard_map/reshape | solution.py:43
  7.8 2.0 %copy.43 = bf16[16,8,16,128]{3,1,0,2:T(8,128)(2,1)} copy(bf16[16,8,16,128]{3,2,1,0:T(8,128)(2,1)} %reshape.150) | data formatting | bytes 1048576 | tf_op jit(solution)/shard_map/reshape | solution.py:43
  9.8 7.4 %all-to-all-start = ((bf16[16,8,16,128]{3,1,0,2:T(8,128)(2,1)}), bf16[16,8,16,128]{3,1,0,2:T(8,128)(2,1)}, u32[]{:S(2)}, u32[]{:S(2)}) async-start(bf16[16,8,16,128]{3,1,0,2:T(8,128)(2,1)} %copy.43), calls=%async_computation | async-start | bytes 1048576 | tf_op jit(solution)/shard_map/all_to_all | solution.py:44
  17.2 0.0 copy-done.1
  17.2 0.0 copy-start.5
  17.2 0.0 copy-start.8
  17.2 0.3 convert_reduce_fusion
  17.6 1.0 %fusion.2 = f32[16,128]{1,0:T(8,128)S(1)} fusion(bf16[16,128,512]{2,1,0:T(8,128)(2,1)S(1)} %copy-done.1, f32[16,128]{1,0:T(8,128)S(1)} %broadcast_multiply_fusion), kind=kLoop, calls=%fused_computation.7 | loop fusion | flops 4192256 | bytes 2113536 | tf_op jit(solution)/shard_map/reduce_sum | solution.py:15
  18.6 0.0 copy-done.5
  18.6 0.1 copy.47
  18.7 0.0 copy-done.8
  18.7 0.0 copy-start.7
  18.8 4.4 %fusion.25 = bf16[16,8,16,128]{3,2,1,0:T(8,128)(2,1)} fusion(bf16[16,128,512]{2,1,0:T(8,128)(2,1)S(1)} %copy-done.1, f32[512]{0:T(512)S(1)} %copy-done.8, f32[16,128]{1,0:T(8,128)S(1)} %add_rsqrt_fusion, f32[16,128]{1,0:T(8,128)S(1)} %broadcast_multiply_fusion, bf16[512,512]{1,0:T(8,128)(2,1)} %param.20, bf16[512,16,8]{0,2,1:T(8,128)(2,1)S(1)} %bitcast.102), kind=kOutput, calls=%fused_computation.30 | convolution fusion | flops 1352925184 | bytes 3295232 | tf_op jit(solution)/shard_map/enh,hjc->ecjn/dot_general | solution.py:50
  23.1 0.0 copy-done.7
  23.1 0.0 copy-start.3
  23.1 0.1 copy.46
  23.2 2.0 %copy.49 = bf16[16,8,16,128]{3,1,0,2:T(8,128)(2,1)} copy(bf16[16,8,16,128]{3,2,1,0:T(8,128)(2,1)} %fusion.25) | data formatting | bytes 1048576 | tf_op jit(solution)/shard_map/convert_element_type | solution.py:52
  25.3 0.8 %sort.17 = (s32[32,1]{1,0:T(8,128)}, s32[32,1]{1,0:T(8,128)S(1)}) sort(s32[32,1]{1,0:T(8,128)S(1)} %copy.46, s32[32,1]{1,0:T(8,128)S(1)} %iota.7), dimensions={0}, to_apply=%region_2.3 | sort | flops 160 | bytes 512 | tf_op jit(solution)/shard_map/jit(argsort)/sort | solution.py:68
  26.1 0.1 reduce.2
  26.2 5.3 %all-to-all-done = bf16[16,8,16,128]{3,1,0,2:T(8,128)(2,1)} async-done(((bf16[16,8,16,128]{3,1,0,2:T(8,128)(2,1)}), bf16[16,8,16,128]{3,1,0,2:T(8,128)(2,1)}, u32[]{:S(2)}, u32[]{:S(2)}) %all-to-all-start) | async-done | bytes 524320 | tf_op jit(solution)/shard_map/all_to_all | solution.py:44
  31.5 4.2 %all-to-all-start.1 = ((bf16[16,8,16,128]{3,1,0,2:T(8,128)(2,1)}), bf16[16,8,16,128]{3,1,0,2:T(8,128)(2,1)S(1)}, u32[]{:S(2)}, u32[]{:S(2)}) async-start(bf16[16,8,16,128]{3,1,0,2:T(8,128)(2,1)} %copy.49), calls=%async_computation.1 | async-start | bytes 1048576 | tf_op jit(solution)/shard_map/all_to_all | solution.py:65
  35.7 0.0 copy-done.3
  35.7 0.6 %gather_fusion.1 = bf16[32,128,64]{1,2,0:T(8,128)(2,1)S(1)} fusion(bf16[32,1,128,64]{2,3,1,0:T(8,128)(2,1)S(1)} %copy-done.3, s32[32]{0:T(128)S(1)} %or_bitcast_fusion), kind=kCustom, calls=%fused_computation.1 | custom fusion | bytes 1048832 | tf_op jit(solution)/shard_map/gather | solution.py:70
  36.4 1.1 %fusion.16 = f32[16,128]{1,0:T(8,128)S(1)} fusion(bf16[16,8,16,128]{3,1,0,2:T(8,128)(2,1)} %all-to-all-done), kind=kLoop, calls=%fused_computation.27 | loop fusion | flops 522240 | bytes 532480 | tf_op jit(solution)/shard_map/reduce_sum | solution.py:13
  37.6 1.2 %fusion.31 = f32[16,128]{1,0:T(8,128)S(1)} fusion(f32[16,128]{1,0:T(8,128)S(1)} %broadcast_multiply_fusion.1, bf16[16,8,16,128]{3,1,0,2:T(8,128)(2,1)} %all-to-all-done), kind=kLoop, calls=%fused_computation.32 | loop fusion | flops 1046528 | bytes 540672 | tf_op jit(solution)/shard_map/reduce_sum | solution.py:15
  38.8 11.2 %all-to-all-done.1 = bf16[16,8,16,128]{3,1,0,2:T(8,128)(2,1)S(1)} async-done(((bf16[16,8,16,128]{3,1,0,2:T(8,128)(2,1)}), bf16[16,8,16,128]{3,1,0,2:T(8,128)(2,1)S(1)}, u32[]{:S(2)}, u32[]{:S(2)}) %all-to-all-start.1) | async-done | bytes 524320 | tf_op jit(solution)/shard_map/all_to_all | solution.py:65
  50.0 0.3 copy.50
  50.3 0.4 reshape.153
  50.7 1.4 %copy.51 = bf16[16,8,32,64]{3,1,2,0:T(8,128)(2,1)} copy(bf16[16,8,32,64]{3,2,1,0:T(8,128)(2,1)S(1)} %reshape.153) | data formatting | bytes 1048576 | tf_op jit(solution)/shard_map/reshape | solution.py:67
  52.1 2.2 %gather_fusion.2 = bf16[32,16,8,64]{3,2,1,0:T(8,128)(2,1)S(1)} fusion(bf16[16,8,32,64]{3,1,2,0:T(8,128)(2,1)} %copy.51, s32[1024]{0:T(1024)S(1)} %pad_clamp_fusion), kind=kCustom, calls=%fused_computation.2 | custom fusion | bytes 1048704 | tf_op jit(solution)/shard_map/jit(_take)/gather | solution.py:69
  54.3 0.2 select_bitcast_fusion
  54.5 0.4 fusion.15
  54.9 0.0 copy-start.4
  54.9 0.0 copy-start.6
  54.9 0.7 %copy.53 = bf16[16,8,32,128]{3,2,1,0:T(8,128)(2,1)S(1)} copy(bf16[16,8,32,128]{3,0,1,2:T(8,128)(2,1)S(1)} %fusion.15) | data formatting | bytes 2097152 | tf_op jit(solution)/shard_map/convert_element_type | solution.py:72
  55.6 1.3 %reshape.154 = bf16[16,8,4096]{2,1,0:T(8,128)(2,1)} reshape(bf16[16,8,32,128]{3,2,1,0:T(8,128)(2,1)S(1)} %copy.53) | data formatting | bytes 2097152 | tf_op jit(solution)/shard_map/reshape | solution.py:72
  56.9 0.0 copy-done.4
  56.9 0.0 copy-done.6
  56.9 1.8 %convolution_convert_fusion = bf16[16,128,512]{2,1,0:T(8,128)(2,1)S(1)} fusion(f32[128]{0:T(128)S(1)} %copy-done.6, f32[16,128]{1,0:T(8,128)S(1)} %add_rsqrt_fusion.1, f32[16,128]{1,0:T(8,128)S(1)} %broadcast_multiply_fusion.1, bf16[16,8,16,128]{3,1,0,2:T(8,128)(2,1)} %all-to-all-done, bf16[128,512]{1,0:T(8,128)(2,1)S(1)} %copy-done.4), kind=kOutput, calls=%fused_computation.19 | convolution fusion | flops 270794752 | bytes 2769408 | tf_op jit(solution)/shard_map/ecn,ch->enh/dot_general | solution.py:55
  58.8 5.2 %add_convert_fusion = bf16[16,128,512]{2,1,0:T(8,128)(2,1)} fusion(bf16[16,128,512]{2,1,0:T(8,128)(2,1)S(1)} %convolution_convert_fusion, bf16[512,512]{1,0:T(8,128)(2,1)} %param.18, bf16[512,512]{1,0:T(8,128)(2,1)} %param.17), kind=kOutput, calls=%fused_computation.11 | convolution fusion | flops 2155872256 | bytes 5242880 | tf_op jit(solution)/shard_map/enh,hg->eng/dot_general | solution.py:61
  (11 shorter events, 0.1 us)
Async XLA Ops:
  0.6 1.5 %copy-start = (bf16[16,8,4096]{2,1,0:T(8,128)(2,1)S(1)}, bf16[16,8,4096]{2,1,0:T(8,128)(2,1)}, u32[]{:S(2)}) copy-start(bf16[16,8,4096]{2,1,0:T(8,128)(2,1)} %param.11) | copy-start | bytes 3145732
  0.6 2.4 %copy-start.2 = (bf16[32,1,128,64]{2,3,1,0:T(8,128)(2,1)S(1)}, bf16[32,1,128,64]{2,3,1,0:T(8,128)(2,1)}, u32[]{:S(2)}) copy-start(bf16[32,1,128,64]{2,3,1,0:T(8,128)(2,1)} %param.13) | copy-start | bytes 1572868
  5.2 12.0 %copy-start.1 = (bf16[16,128,512]{2,1,0:T(8,128)(2,1)S(1)}, bf16[16,128,512]{2,1,0:T(8,128)(2,1)}, u32[]{:S(2)}) copy-start(bf16[16,128,512]{2,1,0:T(8,128)(2,1)} %param.12) | copy-start | bytes 6291460
  9.8 21.8 %all-to-all-start = ((bf16[16,8,16,128]{3,1,0,2:T(8,128)(2,1)}), bf16[16,8,16,128]{3,1,0,2:T(8,128)(2,1)}, u32[]{:S(2)}, u32[]{:S(2)}) async-start(bf16[16,8,16,128]{3,1,0,2:T(8,128)(2,1)} %copy.43), calls=%async_computation | async-start | bytes 1048576 | tf_op jit(solution)/shard_map/all_to_all | solution.py:44
  17.2 1.4 %copy-start.5 = (bf16[512,128]{1,0:T(8,128)(2,1)S(1)}, bf16[512,128]{1,0:T(8,128)(2,1)}, u32[]{:S(2)}) copy-start(bf16[512,128]{1,0:T(8,128)(2,1)} %param.21) | copy-start | bytes 393220
  17.2 1.5 %copy-start.8 = (f32[512]{0:T(512)S(1)}, f32[512]{0:T(512)}, u32[]{:S(2)}) copy-start(f32[512]{0:T(512)} %param.19) | copy-start | bytes 6148
  18.7 4.4 %copy-start.7 = (s32[32,1]{0,1:T(1,128)S(1)}, s32[32,1]{0,1:T(1,128)}, u32[]{:S(2)}) copy-start(s32[32,1]{0,1:T(1,128)} %param.14) | copy-start | bytes 388
  23.1 12.6 %copy-start.3 = (bf16[32,1,128,64]{2,3,1,0:T(8,128)(2,1)S(1)}, bf16[32,1,128,64]{2,3,1,0:T(8,128)(2,1)}, u32[]{:S(2)}) copy-start(bf16[32,1,128,64]{2,3,1,0:T(8,128)(2,1)} %param.13) | copy-start | bytes 1572868
  31.5 18.4 %all-to-all-start.1 = ((bf16[16,8,16,128]{3,1,0,2:T(8,128)(2,1)}), bf16[16,8,16,128]{3,1,0,2:T(8,128)(2,1)S(1)}, u32[]{:S(2)}, u32[]{:S(2)}) async-start(bf16[16,8,16,128]{3,1,0,2:T(8,128)(2,1)} %copy.49), calls=%async_computation.1 | async-start | bytes 1048576 | tf_op jit(solution)/shard_map/all_to_all | solution.py:65
  54.9 2.0 %copy-start.4 = (bf16[128,512]{1,0:T(8,128)(2,1)S(1)}, bf16[128,512]{1,0:T(8,128)(2,1)}, u32[]{:S(2)}) copy-start(bf16[128,512]{1,0:T(8,128)(2,1)} %param.16) | copy-start | bytes 393220
  54.9 2.0 %copy-start.6 = (f32[128]{0:T(128)S(1)}, f32[128]{0:T(128)}, u32[]{:S(2)}) copy-start(f32[128]{0:T(128)} %param.15) | copy-start | bytes 1540
where the time goes:
time: 64.6 us; the launch traced here: 64 us
  waiting for transfers between devices  16.5 us (26%)
  local copies, waits for them, and re-layouts  16.4 us (25%)
  matrix products  12.4 us (19%)
  starting transfers between devices  11.6 us (18%)
  other arithmetic  6.21 us (10%)
  between operations  0.9 us (1%)
    all_to_all x1, waiting for transfers between devices, shards(): lax.all_to_all(decoded_sent, 'ch', split_axis=2, concat_axis=1, tiled=True)  11.2 us
    all_to_all x1, starting transfers between devices, shards(): lax.all_to_all(grid_sent, 'ch', split_axis=2, concat_axis=1, tiled=True)  7.44 us
    all_to_all x1, waiting for transfers between devices, shards(): lax.all_to_all(grid_sent, 'ch', split_axis=2, concat_axis=1, tiled=True)  5.32 us
    dot_general x1, matrix products, shards(): jnp.einsum('enh,hg->eng', middle, enc_out, preferred_element_type=jnp.flo...  5.24 us
    reshape x2, local copies, waits for them, and re-layouts, shards(): grid_vals.astype(jnp.bfloat16)  4.55 us
    dot_general x1, matrix products, shards(): jnp.einsum('enh,hjc->ecjn', middle, out_split, preferred_element_type=jnp...  4.37 us
    all_to_all x1, starting transfers between devices, shards(): lax.all_to_all(decoded_sent, 'ch', split_axis=2, concat_axis=1, tiled=True)  4.17 us
    reduce_sum x2, other arithmetic, normalize(): spread = jnp.mean(centred * centred, axis=along, keepdims=True)  2.17 us
  transfers between devices with their start and end apart: 2, of which 2 were waited for; matrix products, arithmetic and copies ran while one was open for 19% of the time, Pallas kernels for 0%

commit v1 on v0

--- a/solution.py
+++ b/solution.py
@@ -62,7 +62,9 @@
         "enh,hg->eng", middle, enc_out, preferred_element_type=jnp.float32
     )
     latent_a = result.astype(jnp.bfloat16)
-    received_b = lax.all_to_all(decoded_sent, "ch", split_axis=2, concat_axis=1, tiled=True)
+    cells = jnp.split(decoded_sent, lax.axis_size("ch"), axis=2)
+    received = lax.all_to_all(jnp.stack(cells), "ch", 0, 0)
+    received_b = jnp.concatenate(received, axis=1)
     arranged = received_b.reshape(samples, groups, own_channels, node_rows)
     node_blocks = jnp.moveaxis(arranged, 1, 2).reshape(samples, own_channels, blocks_all, BN)
     inverse = jnp.argsort(cell_tiles, axis=0).T

time: 64.6 us -> 74.1 us (1.15)
  local copies, waits for them, and re-layouts: 16.4 us -> 29.4 us
  waiting for transfers between devices: 16.5 us -> 11.2 us
  starting transfers between devices: 11.6 us -> 13.4 us
    unnamed x20 -> x33, local copies, waits for them, and re-layouts: 0.26 us -> 10.3 us
    all_to_all x1, waiting for transfers between devices: 5.32 us -> 0.01 us  [shards(): lax.all_to_all(grid_sent, 'ch', split_axis=2, concat_axis=1, tiled=True)]
    split x0 -> x1, local copies, waits for them, and re-layouts: none -> 4.4 us  [shards(): cells = jnp.split(decoded_sent, lax.axis_size('ch'), axis=2)]
    convert_element_type x1 -> x0, local copies, waits for them, and re-layouts: 2.04 us -> none  [shards(): decoded_sent = jnp.einsum('enh,hjc->ecjn', middle, out_split, preferred_e...]
    all_to_all x1, starting transfers between devices: 4.17 us -> 5.96 us  [shards(): received = lax.all_to_all(jnp.stack(cells), 'ch', 0, 0)]
  transfers between devices with their start and end apart: 2 -> 2, of which waited for: 2 -> 1; matrix products, arithmetic and copies ran while one was open for 19% -> 32% of each run, Pallas kernels for 0% -> 0%
where the time goes in v1:
time: 74.1 us; the launch traced here: 73.4 us
  local copies, waits for them, and re-layouts  29.4 us (40%)
  starting transfers between devices  13.4 us (18%)
  matrix products  12.4 us (17%)
  waiting for transfers between devices  11.2 us (15%)
  other arithmetic  6.09 us (8%)
  between operations  0.9 us (1%)
    all_to_all x1, waiting for transfers between devices, shards(): received = lax.all_to_all(jnp.stack(cells), 'ch', 0, 0)  11.2 us
    unnamed x33, local copies, waits for them, and re-layouts  10.3 us
    all_to_all x1, starting transfers between devices, shards(): lax.all_to_all(grid_sent, 'ch', split_axis=2, concat_axis=1, tiled=True)  7.44 us
    all_to_all x1, starting transfers between devices, shards(): received = lax.all_to_all(jnp.stack(cells), 'ch', 0, 0)  5.96 us
    dot_general x1, matrix products, shards(): jnp.einsum('enh,hg->eng', middle, enc_out, preferred_element_type=jnp.flo...  5.25 us
    reshape x2, local copies, waits for them, and re-layouts, shards(): grid_vals.astype(jnp.bfloat16)  4.55 us
    split x1, local copies, waits for them, and re-layouts, shards(): cells = jnp.split(decoded_sent, lax.axis_size('ch'), axis=2)  4.4 us
    dot_general x1, matrix products, shards(): jnp.einsum('enh,hjc->ecjn', middle, out_split, preferred_element_type=jnp...  4.37 us
  transfers between devices with their start and end apart: 2, of which 1 were waited for; matrix products, arithmetic and copies ran while one was open for 32% of the time, Pallas kernels for 0%

profile of v1, /device:TPU:0, one launch (start us, length us, event | category | flops | bytes accessed | tf_op | source)
XLA Modules:
  0.0 73.4 jit_solution(10340148514329407295)
XLA Ops:
  0.6 0.0 copy-start
  0.6 0.0 copy-start.2
  0.7 0.9 %copy.298 = s32[32,1]{1,0:T(8,128)S(1)} copy(s32[32,1]{0,1:T(1,128)} %param.14) | data formatting | bytes 256 | tf_op args[3]
  1.5 0.7 fusion.60
  2.2 0.7 and_bitcast_fusion
  2.8 0.8 %sort.17 = (s32[32,1]{1,0:T(8,128)}, s32[32,1]{1,0:T(8,128)S(1)}) sort(s32[32,1]{1,0:T(8,128)S(1)} %copy.298, s32[32,1]{1,0:T(8,128)S(1)} %iota.7), dimensions={0}, to_apply=%region_2.3 | sort | flops 160 | bytes 512 | tf_op jit(solution)/shard_map/jit(argsort)/sort | solution.py:70
  3.6 0.1 reduce.2
  3.8 0.0 copy-done
  3.8 0.9 %gather_fusion = bf16[32,16,8,128]{3,2,1,0:T(8,128)(2,1)S(1)} fusion(bf16[16,8,32,128]{3,1,2,0:T(8,128)(2,1)S(1)} %bitcast.138, s32[1024]{0:T(1024)S(1)} %get-tuple-element.23), kind=kCustom, calls=%fused_computation | custom fusion | bytes 2097280 | tf_op jit(solution)/shard_map/jit(_take)/gather | solution.py:40
  4.7 0.0 copy-done.2
  4.7 0.5 fusion.14
  5.2 1.6 %copy.294 = bf16[16,8,32,64]{3,2,1,0:T(8,128)(2,1)} copy(bf16[16,8,32,64]{3,1,0,2:T(8,128)(2,1)S(1)} %fusion.14) | data formatting | bytes 1048576 | tf_op jit(solution)/shard_map/convert_element_type | solution.py:43
  6.9 0.0 copy-start.1
  6.9 2.6 %reshape.151 = bf16[16,8,16,128]{3,2,1,0:T(8,128)(2,1)} reshape(bf16[16,8,32,64]{3,2,1,0:T(8,128)(2,1)} %copy.294) | data formatting | bytes 1048576 | tf_op jit(solution)/shard_map/reshape | solution.py:43
  9.5 2.0 %copy.295 = bf16[16,8,16,128]{3,1,0,2:T(8,128)(2,1)} copy(bf16[16,8,16,128]{3,2,1,0:T(8,128)(2,1)} %reshape.151) | data formatting | bytes 1048576 | tf_op jit(solution)/shard_map/reshape | solution.py:43
  11.4 7.4 %all-to-all-start = ((bf16[16,8,16,128]{3,1,0,2:T(8,128)(2,1)}), bf16[16,8,16,128]{3,1,0,2:T(8,128)(2,1)}, u32[]{:S(2)}, u32[]{:S(2)}) async-start(bf16[16,8,16,128]{3,1,0,2:T(8,128)(2,1)} %copy.295), calls=%async_computation | async-start | bytes 1048576 | tf_op jit(solution)/shard_map/all_to_all | solution.py:44
  18.9 0.0 copy-done.1
  18.9 0.0 copy-start.5
  18.9 0.0 copy-start.7
  18.9 0.3 convert_reduce_fusion
  19.3 1.0 %fusion.2 = f32[16,128]{1,0:T(8,128)S(1)} fusion(bf16[16,128,512]{2,1,0:T(8,128)(2,1)S(1)} %copy-done.1, f32[16,128]{1,0:T(8,128)S(1)} %broadcast_multiply_fusion), kind=kLoop, calls=%fused_computation.7 | loop fusion | flops 4192256 | bytes 2113536 | tf_op jit(solution)/shard_map/reduce_sum | solution.py:15
  20.3 0.0 copy-done.5
  20.3 0.1 copy.299
  20.4 0.0 copy-done.7
  20.4 4.4 %fusion.25 = bf16[16,8,16,128]{3,2,1,0:T(8,128)(2,1)} fusion(bf16[16,128,512]{2,1,0:T(8,128)(2,1)S(1)} %copy-done.1, f32[512]{0:T(512)S(1)} %copy-done.7, f32[16,128]{1,0:T(8,128)S(1)} %add_rsqrt_fusion, f32[16,128]{1,0:T(8,128)S(1)} %broadcast_multiply_fusion, bf16[512,512]{1,0:T(8,128)(2,1)} %param.20, bf16[512,16,8]{0,2,1:T(8,128)(2,1)S(1)} %bitcast.140), kind=kOutput, calls=%fused_computation.30 | convolution fusion | flops 1352925184 | bytes 3295232 | tf_op jit(solution)/shard_map/enh,hjc->ecjn/dot_general | solution.py:50
  24.8 0.0 copy-start.3
  24.8 4.4 %fusion.62 = (bf16[16,8,1,128]{3,2,1,0:T(2,128)(2,1)S(1)}, bf16[16,8,1,128]{3,2,1,0:T(2,128)(2,1)S(1)}, bf16[16,8,1,128]{3,2,1,0:T(2,128)(2,1)S(1)}, bf16[16,8,1...) fusion(bf16[16,8,16,128]{3,2,1,0:T(8,128)(2,1)} %fusion.25), kind=kLoop, calls=%fused_computation.90 | loop fusion | bytes 1048576 | tf_op jit(solution)/shard_map/split | solution.py:65
  29.2 0.6 constant_dynamic-update-slice_fusion.15
  29.8 0.6 constant_dynamic-update-slice_fusion.14
  30.4 0.6 constant_dynamic-update-slice_fusion.13
  31.1 0.6 constant_dynamic-update-slice_fusion.12
  31.7 0.6 constant_dynamic-update-slice_fusion.11
  32.3 0.6 constant_dynamic-update-slice_fusion.10
  32.9 0.6 constant_dynamic-update-slice_fusion.9
  33.5 0.6 constant_dynamic-update-slice_fusion.8
  34.2 0.6 constant_dynamic-update-slice_fusion.7
  34.8 0.6 constant_dynamic-update-slice_fusion.6
  35.4 0.6 constant_dynamic-update-slice_fusion.5
  36.0 0.6 constant_dynamic-update-slice_fusion.4
  36.6 0.6 constant_dynamic-update-slice_fusion.3
  37.3 0.6 constant_dynamic-update-slice_fusion.2
  37.9 0.6 constant_dynamic-update-slice_fusion.1
  38.5 0.6 constant_dynamic-update-slice_fusion
  39.1 0.0 all-to-all-done
  39.1 6.0 %all-to-all-start.1 = ((bf16[16,16,8,1,128]{4,2,1,3,0:T(8,128)(2,1)}), bf16[16,16,8,1,128]{4,2,1,3,0:T(8,128)(2,1)S(1)}, u32[]{:S(2)}, u32[]{:S(2)}) async-start(bf16[16,16,8,1,128]{4,2,1,3,0:T(8,128)(2,1)} %constant_dynamic-update-slice_fusion), calls=%async_computation.1 | async-start | bytes 1048576 | tf_op jit(solution)/shard_map/all_to_all | solution.py:66
  45.1 0.0 copy-done.3
  45.1 0.6 gather_fusion.1
  45.8 1.1 %fusion.16 = f32[16,128]{1,0:T(8,128)S(1)} fusion(bf16[16,8,16,128]{3,1,0,2:T(8,128)(2,1)} %all-to-all-done), kind=kLoop, calls=%fused_computation.27 | loop fusion | flops 522240 | bytes 532480 | tf_op jit(solution)/shard_map/reduce_sum | solution.py:13
  46.9 1.2 %fusion.31 = f32[16,128]{1,0:T(8,128)S(1)} fusion(f32[16,128]{1,0:T(8,128)S(1)} %broadcast_multiply_fusion.1, bf16[16,8,16,128]{3,1,0,2:T(8,128)(2,1)} %all-to-all-done), kind=kLoop, calls=%fused_computation.32 | loop fusion | flops 1046528 | bytes 540672 | tf_op jit(solution)/shard_map/reduce_sum | solution.py:15
  48.1 11.2 %all-to-all-done.1 = bf16[16,16,8,1,128]{4,2,1,3,0:T(8,128)(2,1)S(1)} async-done(((bf16[16,16,8,1,128]{4,2,1,3,0:T(8,128)(2,1)}), bf16[16,16,8,1,128]{4,2,1,3,0:T(8,128)(2,1)S(1)}, u32[]{:S(2)}, u32[]{:S(2)}) %all-to-all-start.1) | async-done | bytes 524320 | tf_op jit(solution)/shard_map/all_to_all | solution.py:66
  59.4 0.3 copy.301
  59.7 0.4 reshape.155
  60.1 1.4 %copy.302 = bf16[16,8,32,64]{3,1,2,0:T(8,128)(2,1)} copy(bf16[16,8,32,64]{3,2,1,0:T(8,128)(2,1)S(1)} %reshape.155) | data formatting | bytes 1048576 | tf_op jit(solution)/shard_map/reshape | solution.py:69
  61.5 2.2 %gather_fusion.2 = bf16[32,16,8,64]{3,2,1,0:T(8,128)(2,1)S(1)} fusion(bf16[16,8,32,64]{3,1,2,0:T(8,128)(2,1)} %copy.302, s32[1024]{0:T(1024)S(1)} %get-tuple-element.22), kind=kCustom, calls=%fused_computation.2 | custom fusion | bytes 1048704 | tf_op jit(solution)/shard_map/jit(_take)/gather | solution.py:71
  63.7 0.2 select_bitcast_fusion
  63.9 0.4 fusion.15
  64.3 0.0 copy-start.4
  64.3 0.0 copy-start.6
  64.3 0.7 copy.304
  65.0 1.3 %reshape.156 = bf16[16,8,4096]{2,1,0:T(8,128)(2,1)} reshape(bf16[16,8,32,128]{3,2,1,0:T(8,128)(2,1)S(1)} %copy.304) | data formatting | bytes 2097152 | tf_op jit(solution)/shard_map/reshape | solution.py:74
  66.3 0.0 copy-done.4
  66.3 0.0 copy-done.6
  66.3 1.8 %convolution_convert_fusion = bf16[16,128,512]{2,1,0:T(8,128)(2,1)S(1)} fusion(f32[128]{0:T(128)S(1)} %copy-done.6, f32[16,128]{1,0:T(8,128)S(1)} %add_rsqrt_fusion.1, f32[16,128]{1,0:T(8,128)S(1)} %broadcast_multiply_fusion.1, bf16[16,8,16,128]{3,1,0,2:T(8,128)(2,1)} %all-to-all-done, bf16[128,512]{1,0:T(8,128)(2,1)S(1)} %copy-done.4), kind=kOutput, calls=%fused_computation.19 | convolution fusion | flops 270794752 | bytes 2769408 | tf_op jit(solution)/shard_map/ecn,ch->enh/dot_general | solution.py:55
  68.1 5.3 %add_convert_fusion = bf16[16,128,512]{2,1,0:T(8,128)(2,1)} fusion(bf16[16,128,512]{2,1,0:T(8,128)(2,1)S(1)} %convolution_convert_fusion, bf16[512,512]{1,0:T(8,128)(2,1)} %param.18, bf16[512,512]{1,0:T(8,128)(2,1)} %param.17), kind=kOutput, calls=%fused_computation.11 | convolution fusion | flops 2155872256 | bytes 5242880 | tf_op jit(solution)/shard_map/enh,hg->eng/dot_general | solution.py:61
  (10 shorter events, 0.1 us)
Async XLA Ops:
  0.6 3.1 %copy-start = (bf16[16,8,4096]{2,1,0:T(8,128)(2,1)S(1)}, bf16[16,8,4096]{2,1,0:T(8,128)(2,1)}, u32[]{:S(2)}) copy-start(bf16[16,8,4096]{2,1,0:T(8,128)(2,1)} %param.11) | copy-start | bytes 3145732
  0.6 4.1 %copy-start.2 = (bf16[32,1,128,64]{2,3,1,0:T(8,128)(2,1)S(1)}, bf16[32,1,128,64]{2,3,1,0:T(8,128)(2,1)}, u32[]{:S(2)}) copy-start(bf16[32,1,128,64]{2,3,1,0:T(8,128)(2,1)} %param.13) | copy-start | bytes 1572868
  6.9 12.0 %copy-start.1 = (bf16[16,128,512]{2,1,0:T(8,128)(2,1)S(1)}, bf16[16,128,512]{2,1,0:T(8,128)(2,1)}, u32[]{:S(2)}) copy-start(bf16[16,128,512]{2,1,0:T(8,128)(2,1)} %param.12) | copy-start | bytes 6291460
  11.4 27.7 %all-to-all-start = ((bf16[16,8,16,128]{3,1,0,2:T(8,128)(2,1)}), bf16[16,8,16,128]{3,1,0,2:T(8,128)(2,1)}, u32[]{:S(2)}, u32[]{:S(2)}) async-start(bf16[16,8,16,128]{3,1,0,2:T(8,128)(2,1)} %copy.295), calls=%async_computation | async-start | bytes 1048576 | tf_op jit(solution)/shard_map/all_to_all | solution.py:44
  18.9 1.4 %copy-start.5 = (bf16[512,128]{1,0:T(8,128)(2,1)S(1)}, bf16[512,128]{1,0:T(8,128)(2,1)}, u32[]{:S(2)}) copy-start(bf16[512,128]{1,0:T(8,128)(2,1)} %param.21) | copy-start | bytes 393220
  18.9 1.5 %copy-start.7 = (f32[512]{0:T(512)S(1)}, f32[512]{0:T(512)}, u32[]{:S(2)}) copy-start(f32[512]{0:T(512)} %param.19) | copy-start | bytes 6148
  24.8 20.3 %copy-start.3 = (bf16[32,1,128,64]{2,3,1,0:T(8,128)(2,1)S(1)}, bf16[32,1,128,64]{2,3,1,0:T(8,128)(2,1)}, u32[]{:S(2)}) copy-start(bf16[32,1,128,64]{2,3,1,0:T(8,128)(2,1)} %param.13) | copy-start | bytes 1572868
  39.1 20.2 %all-to-all-start.1 = ((bf16[16,16,8,1,128]{4,2,1,3,0:T(8,128)(2,1)}), bf16[16,16,8,1,128]{4,2,1,3,0:T(8,128)(2,1)S(1)}, u32[]{:S(2)}, u32[]{:S(2)}) async-start(bf16[16,16,8,1,128]{4,2,1,3,0:T(8,128)(2,1)} %constant_dynamic-update-slice_fusion), calls=%async_computation.1 | async-start | bytes 1048576 | tf_op jit(solution)/shard_map/all_to_all | solution.py:66
  64.3 2.0 %copy-start.4 = (bf16[128,512]{1,0:T(8,128)(2,1)S(1)}, bf16[128,512]{1,0:T(8,128)(2,1)}, u32[]{:S(2)}) copy-start(bf16[128,512]{1,0:T(8,128)(2,1)} %param.16) | copy-start | bytes 393220
  64.3 2.0 %copy-start.6 = (f32[128]{0:T(128)S(1)}, f32[128]{0:T(128)}, u32[]{:S(2)}) copy-start(f32[128]{0:T(128)} %param.15) | copy-start | bytes 1540
